TPU v7x, 32 devices: a whole 2x2x4 slice. The times are simulated.
32 devices in a mesh: gx: 4 (over y, x), gy: 2 (over core), gz: 4 (over z).
Axes of the slice: x: 2, y: 2, z: 4, core: 2. Of those that a mesh axis runs over, the one named last changes fastest.
Arguments:
- positions: float32 [3, 4, 8, 16, 64], P(None, 'gz', 'gx', 'gy'), may hold values from 0 to 1
- counts: int32 [4, 8, 16], P('gz', 'gx', 'gy'), may hold values from 16 to 64, as said below
Outputs:
- force: float32 [3, 4, 8, 16, 64], P(None, 'gz', 'gx', 'gy')
- energy: float32 [4, 8, 16, 64], P('gz', 'gx', 'gy')
Inputs may be any that keep to these rules, and one draw needn't show every extreme that they name: `counts`: every draw has some full cells.
All inputs are finite; a program needn't handle non-finite values.
Results may differ from a plain program's by a relative error of at most 0.0003.
Values sent between devices are 32-bit elements; how exact they have to be, the bound alone decides.
A program may use at most 64 MiB of HBM per device.

v0:
```python
import functools
import math

import jax
import jax.numpy as jnp
from jax import lax
from jax.experimental import pallas as pl
from jax.experimental.pallas import tpu as pltpu
from jax.sharding import PartitionSpec as P

CUT = 4.95
SIDES = (12.0, 12.0, 2.5)
FAR = 1024.0
LOG2E = math.log2(math.e)
SCALE = math.sqrt(LOG2E / 8.0)
REACH = CUT * CUT * LOG2E / 8.0
SPLIT = 0.5
SLIDES = tuple(side * SCALE for side in SIDES)
A = 2.0 * LOG2E
B = 0.75 * LOG2E
G1 = 2.0 ** (-REACH) / REACH**2
G2 = 2.0 ** (-REACH * 8.0 / 3.0) / REACH**2
SIGMA = (3.0 / 16.0) * G1 / G2
CLASSES = 4
SUB = 8
STATIC = 8
VMEM_BYTES = 67_043_328
SPARE = 16384
DEPTH = 2
LAYERS = 2 * DEPTH + 1
VMEM = pl.BlockSpec(memory_space=pltpu.VMEM)
HBM = pl.BlockSpec(memory_space=pltpu.HBM)


AXES = ("gz", "gx", "gy")


def layer_slots(nz):
    kept = []
    for a in range(-DEPTH, DEPTH + 1):
        if all((a - k) % nz for k in kept):
            kept.append(a)
    slot = [
        next(i for i, k in enumerate(kept) if (a - k) % nz == 0)
        for a in range(-DEPTH, DEPTH + 1)
    ]
    return kept, slot


def displacements(sizes):
    kept, _ = layer_slots(sizes[0])
    copies, others = [], []
    for s, a in enumerate(kept):
        for b in (-1, 0, 1):
            for c in (-1, 0, 1):
                if (a, b, c) == (0, 0, 0):
                    continue
                step = tuple(-o % n for o, n in zip((a, b, c), sizes))
                copies.append((s, b, c, step))
                if any(step) and step not in others:
                    others.append(step)
    return copies, others


def device(step, sizes):
    return {
        axis: lax.rem(lax.axis_index(axis) + d, n)
        for axis, d, n in zip(AXES, step, sizes)
    }


def enter(sizes):
    _, others = displacements(sizes)
    barrier = pltpu.get_barrier_semaphore()
    for step in others:
        pl.semaphore_signal(
            barrier,
            inc=1,
            device_id=device(step, sizes),
            device_id_type=pl.DeviceIdType.MESH,
        )
    return barrier, len(others)


def edge(offset, length):
    if offset == 0:
        return pl.ds(0, length), pl.ds(1, length)
    if offset < 0:
        return pl.ds(length - 1, 1), pl.ds(0, 1)
    return pl.ds(0, 1), pl.ds(length + 1, 1)


def link(sizes, rx, nt, own, ext, send, recv, s, b, c, step):
    (sx, dx), (st, dt) = edge(b, rx), edge(c, nt)
    source, target = own.at[sx, st], ext.at[s, dx, dt]
    j = 3 * (b + 1) + c + 1
    if not any(step):
        return pltpu.make_async_copy(source, target, recv.at[s, j])
    return pltpu.make_async_remote_copy(
        src_ref=source,
        dst_ref=target,
        send_sem=send.at[s, j],
        recv_sem=recv.at[s, j],
        device_id=device(step, sizes),
        device_id_type=pl.DeviceIdType.MESH,
    )


def start_copies(sizes, rx, nt, own, ext, send, recv):
    copies, _ = displacements(sizes)
    started = []
    for s, b, c, step in copies:
        copy = link(sizes, rx, nt, own, ext, send, recv, s, b, c, step)
        copy.start()
        if any(step):
            started.append(copy)
    return started


def wait_layer(sizes, rx, nt, own, ext, send, recv, slot, a):
    for b in (-1, 0, 1):
        for c in (-1, 0, 1):
            if a is None:
                step = (1, 0, 0)
            else:
                if (a, b, c) == (0, 0, 0):
                    continue
                step = tuple(-o % n for o, n in zip((a, b, c), sizes))
            copy = link(sizes, rx, nt, own, ext, send, recv, slot, b, c, step)
            if any(step):
                copy.wait_recv()
            else:
                copy.wait()


def arrival_order(nz):
    _, slots = layer_slots(nz)
    if nz < 4:
        return [(slots[a + DEPTH], a, a + DEPTH, a) for a in (0, 1, -1, 2, -2)]
    near = jnp.where(lax.axis_index("gz") == nz - 1, -1, 1)
    return [
        (slots[DEPTH], 0, DEPTH, 0),
        (near + DEPTH, near, near + DEPTH, None),
        (slots[0], -2, 0, -2),
        (slots[2 * DEPTH], 2, 2 * DEPTH, 2),
        (DEPTH - near, -near, DEPTH - near, None),
    ]


def iota(shape, dim):
    return lax.broadcasted_iota(jnp.int32, shape, dim)


def group_count(half):
    return (half + CLASSES * (SUB - 1)) // SUB


def load_rows(rx, nt, half, home, count_ref, pos_ref, own, ext, raw):
    lane = iota((1, 2 * half), 1)
    for x in range(rx):
        for t in range(nt):
            n0, n1 = count_ref[0, x, 2 * t], count_ref[0, x, 2 * t + 1]
            occupied = jnp.where(lane < half, lane - n0, lane - half - n1) < 0
            for c in range(3):
                rows = [pos_ref[c, 0, x, 2 * t + k : 2 * t + k + 1, :] for k in (0, 1)]
                row = jnp.concatenate(rows, axis=1)
                raw[c, pl.ds(x * nt + t, 1)] = jnp.where(occupied, row, FAR)
                row = jnp.where(occupied, row * SLIDES[c], FAR)
                own[x, t, c] = row
                ext[home, x + 1, t + 1, c] = row


def assign_slots(tiles, half, raw, slot_ref, cent_row, packed):
    width = 2 * half
    u, v, w = raw[0], raw[1], raw[2]
    here = u < 0.5 * FAR
    xhi, yhi = u >= SPLIT, v >= SPLIT
    masks = [
        here & ~xhi & ~yhi,
        here & ~xhi & yhi,
        here & xhi & ~yhi,
        here & xhi & yhi,
    ]
    ones = [jnp.where(m, 1.0, 0.0) for m in masks]
    i, j = iota((width, width), 0), iota((width, width), 1)
    same = i // half == j // half
    before = jnp.where(same & (i < j), 1.0, 0.0)
    whole = jnp.where(same, 1.0, 0.0)
    stacked = jnp.concatenate(ones, axis=0)
    ranks = jnp.dot(stacked, before, preferred_element_type=jnp.float32)
    totals = jnp.dot(stacked, whole, preferred_element_type=jnp.float32)
    upper = iota((tiles, width), 1) >= half
    slot = jnp.where(here, jnp.where(upper, float(width), 0.0), -2.0 * width)
    ends = jnp.zeros((tiles, width), jnp.float32)
    pack = jnp.zeros((tiles, width), jnp.float32)
    for k in range(CLASSES):
        rank, total = ranks[k * tiles : (k + 1) * tiles], totals[k * tiles : (k + 1) * tiles]
        slot = slot + ones[k] * (ends * SUB + rank)
        ends = ends + jnp.floor((total + (SUB - 1)) * (1.0 / SUB))
        pack = pack + ends * float(16**k)
    px = u * SLIDES[0] + jnp.where(xhi, 0.0, SLIDES[0])
    py = v * SLIDES[1] + jnp.where(yhi, 0.0, SLIDES[1])
    pz = w * SLIDES[2]
    for r in range(tiles):
        slot_ref[r] = slot[r : r + 1]
        packed[r] = pack[r : r + 1]
        for c, p in enumerate((px, py, pz)):
            cent_row[r, c] = p[r : r + 1]


def group_code(packed, r, k, half):
    lane = iota((1, 2 * half), 1)
    return jnp.sum(jnp.where(lane == k * half, packed[r], 0.0)).astype(jnp.int32)


def group_base(code, x, j, g, ry):
    b1, b2, b3 = code & 15, (code >> 4) & 15, (code >> 8) & 15
    xhi = jnp.where(b2 <= g, 1, 0)
    yhi = jnp.where(b3 <= g, 1, jnp.where(b2 <= g, 0, jnp.where(b1 <= g, 1, 0)))
    return (x + xhi) * (ry + 1) + j + yhi


def spread_centres(tiles, nt, ry, half, groups, stride, slot_ref, cent_row, packed, cen, meta):
    width = 2 * half
    sub = iota((SUB, width), 0).astype(jnp.float32)
    upper = jnp.where(iota((SUB, width), 1) >= half, SLIDES[1], 0.0)

    def step(r, carry):
        slot = slot_ref[r]
        rows = [cent_row[r, c] for c in range(3)]
        x, t = r // nt, r % nt
        for k in (0, 1):
            code = group_code(packed, r, k, half)
            for g in range(groups):
                i = (2 * r + k) * stride + g
                meta[i] = group_base(code, x, 2 * t + k, g, ry)
                pick = slot == sub + float(k * width + g * SUB)
                for c in range(3):
                    column = jnp.sum(jnp.where(pick, rows[c], 0.0), axis=1, keepdims=True)
                    wide = jnp.broadcast_to(column, (SUB, width))
                    if c == 1:
                        wide = wide - upper
                    cen[i, c] = wide
        return carry

    lax.fori_loop(0, tiles, step, 0)


def build_pairs(s, cols, ry, half, channels, ext, pairs):
    low = iota((1, 2 * half), 1) < half

    def step(x, carry):
        for c in range(channels):
            rows = [ext[s, x, t, c] for t in range(ry // 2 + 2)]
            for p in range(ry + 1):
                if p % 2:
                    row = rows[(p + 1) // 2]
                else:
                    row = pltpu.roll(jnp.where(low, rows[p // 2 + 1], rows[p // 2]), half, 1)
                pairs[s, x * (ry + 1) + p, c] = row
        return carry

    lax.fori_loop(0, cols, step, 0, unroll=2)


def density_layer(first, slot, shift, z, cells, groups, stride, ry, meta, pairs, cen, vs, rho):
    def step(cell, carry):
        for g in range(groups):
            i = cell * stride + g
            base = meta[i]
            x, y, w = cen[i, 0], cen[i, 1], cen[i, 2]
            if shift is not None:
                w = w - shift
            for b in (0, 1):
                qx, qy, qz = (pairs[slot, base + b * (ry + 1), c] for c in range(3))
                dx, dy, dz = x - qx, y - qy, w - qz
                v = jnp.maximum(((REACH - dx * dx) - dy * dy) - dz * dz, 0.0)
                vs[i, z, b] = v
                part = jnp.exp2(v) * (v * v)
                total = part if b == 0 else total + part
                x = x - SLIDES[0]
            rho[i] = total if first else rho[i] + total
        return carry

    lax.fori_loop(0, cells, step, 0, unroll=2)


def slope_pass(tiles, nt, half, groups, stride, slot_ref, rho, cs, root_ref, sown, sext, home):
    width = 2 * half
    sub = iota((SUB, width), 0).astype(jnp.float32)

    def step(r, carry):
        slot = slot_ref[r]
        value = jnp.zeros((SUB, width), jnp.float32)
        for k in (0, 1):
            for g in range(groups):
                i = (2 * r + k) * stride + g
                one_rho = jnp.sum(rho[i], axis=1, keepdims=True) * G1
                value = value + jnp.where(
                    slot == sub + float(k * width + g * SUB), one_rho, 0.0
                )
                one_rho = jnp.broadcast_to(one_rho, (SUB, width))
                cs[i] = (-0.5 * SIGMA) * lax.rsqrt(jnp.maximum(one_rho, 0.5))
        one_rho = jnp.sum(value, axis=0, keepdims=True)
        root = jnp.sqrt(jnp.where(slot >= 0.0, one_rho, 1.0))
        root_ref[r] = root
        row = (-0.5 * SIGMA) / root
        x, t = r // nt, r % nt
        sown[x, t, 0] = row
        sext[home, x + 1, t + 1, 0] = row
        return carry

    lax.fori_loop(0, tiles, step, 0)


def geometry(slots, ry, i, base, pairs, cen):
    x, y, w = cen[i, 0], cen[i, 1], cen[i, 2]
    for z in range(LAYERS):
        a = z - DEPTH
        wz = w - a * SLIDES[2] if a else w
        for b in (0, 1):
            q = [pairs[slots[z], base + b * (ry + 1), c] for c in range(3)]
            xb = x - SLIDES[0] if b else x
            yield z, b, (xb - q[0], y - q[1], wz - q[2])


def pair_terms(v):
    g = jnp.exp2(v) * ((v + A) * v)
    w = v * jnp.exp2(v * (8.0 / 3.0))
    return g, w * (v + B), w * v


def pair_pass(slots, cells, stride, ry, width, meta, pairs, cen, vs, gd, acc_ref):
    def step(cell, carry):
        for g in range(STATIC):
            i = cell * stride + g
            acc = [jnp.zeros((SUB, width), jnp.float32) for _ in range(4)]
            for z, b, d in geometry(slots, ry, i, meta[i], pairs, cen):
                dens, pair, phi = pair_terms(vs[i, z, b])
                for c in range(3):
                    gd[cell * STATIC + g, z, b, c] = dens * d[c]
                    acc[c] = acc[c] + pair * d[c]
                acc[3] = acc[3] + phi
            for c in range(4):
                acc_ref[i, c] = acc[c]
        return carry

    lax.fori_loop(0, cells, step, 0)


def slope_force(layers, cells, stride, ry, meta, spairs, cs, gd, acc_ref):
    def step(cell, carry):
        for g in range(STATIC):
            i = cell * stride + g
            base, sp = meta[i], cs[i]
            acc = [acc_ref[i, c] for c in range(3)]
            for slot, z in layers:
                for b in (0, 1):
                    f = sp + spairs[slot, base + b * (ry + 1), 0]
                    for c in range(3):
                        acc[c] = acc[c] + f * gd[cell * STATIC + g, z, b, c]
            for c in range(3):
                acc_ref[i, c] = acc[c]
        return carry

    lax.fori_loop(0, cells, step, 0)


def step_kernel(
    sizes, rx, nt, half, count_hbm, pos_hbm, slot_ref, packed, cen, pairs, vs, cs, root_ref,
    spairs, acc_ref, count_ref, pos_ref, own, ext, raw, cent_row, meta, rho, sown, sext, gd,
    load, send, recv, send2, recv2,
):
    loads = [
        pltpu.make_async_copy(count_hbm, count_ref, load.at[0]),
        pltpu.make_async_copy(pos_hbm, pos_ref, load.at[1]),
    ]
    for copy in loads:
        copy.start()
    barrier, arrivals = enter(sizes)
    ry, tiles, cells = 2 * nt, rx * nt, 2 * rx * nt
    width = 2 * half
    kept, slots = layer_slots(sizes[0])
    home = slots[DEPTH]
    groups = group_count(half)
    stride = group_stride(half)
    order = arrival_order(sizes[0])
    for copy in loads:
        copy.wait()
    load_rows(rx, nt, half, home, count_ref, pos_ref, own, ext, raw)
    pl.semaphore_wait(barrier, arrivals)
    sends = start_copies(sizes, rx, nt, own, ext, send, recv)
    assign_slots(tiles, half, raw, slot_ref, cent_row, packed)
    spread_centres(tiles, nt, ry, half, groups, stride, slot_ref, cent_row, packed, cen, meta)

    def arrive(e, own_ref, ext_ref, send_sem, recv_sem, channels, pairs_ref):
        slot, _, _, known = order[e]
        seen = [o[0] for o in order[:e] if isinstance(o[0], int)]
        if isinstance(slot, int) and slot in seen:
            return
        wait_layer(sizes, rx, nt, own_ref, ext_ref, send_sem, recv_sem, slot, known)
        build_pairs(slot, rx + 2, ry, half, channels, ext_ref, pairs_ref)

    for e, (slot, a, z, known) in enumerate(order):
        arrive(e, own, ext, send, recv, 3, pairs)
        if known is None:
            shift = a.astype(jnp.float32) * SLIDES[2]
        else:
            shift = known * SLIDES[2] if known else None
        density_layer(
            e == 0, slot, shift, z, cells, groups, stride, ry, meta, pairs, cen, vs, rho
        )
    slope_pass(tiles, nt, half, groups, stride, slot_ref, rho, cs, root_ref, sown, sext, home)
    sends += start_copies(sizes, rx, nt, sown, sext, send2, recv2)
    pair_pass(slots, cells, stride, ry, width, meta, pairs, cen, vs, gd, acc_ref)
    for chunk in ((0, 1), (2, 3), (4,)):
        for e in chunk:
            arrive(e, sown, sext, send2, recv2, 1, spairs)
        layers = [(order[e][0], order[e][2]) for e in chunk]
        slope_force(layers, cells, stride, ry, meta, spairs, cs, gd, acc_ref)
    for copy in sends:
        copy.wait_send()


def finish_kernel(
    slots, rx, nt, half, slot_ref, packed, cen, pairs, vs, cs, root_ref, spairs, acc_ref,
    force_ref, energy_ref, codes, values,
):
    width, ry, tiles = 2 * half, 2 * nt, rx * nt
    stride = group_stride(half)
    sub = iota((SUB, width), 0).astype(jnp.float32)
    for r in range(tiles):
        for k in (0, 1):
            codes[2 * r + k] = group_code(packed, r, k, half)

    def gather(r, carry):
        slot = slot_ref[r]
        total = [jnp.zeros((SUB, width), jnp.float32) for _ in range(4)]
        for k in (0, 1):
            for g in range(STATIC):
                pick = slot == sub + float(k * width + g * SUB)
                for c in range(4):
                    part = jnp.sum(acc_ref[(2 * r + k) * stride + g, c], axis=1, keepdims=True)
                    total[c] = total[c] + jnp.where(pick, part, 0.0)
        for c in range(4):
            values[r, c] = total[c]
        return carry

    lax.fori_loop(0, tiles, gather, 0, unroll=2)

    def rest(cell, carry):
        r, k = cell // 2, cell % 2
        x, j = r // nt, 2 * (r % nt) + k
        code = codes[cell]

        def group(g, carry):
            i = cell * stride + g
            base, sp = group_base(code, x, j, g, ry), cs[i]
            acc = [jnp.zeros((SUB, width), jnp.float32) for _ in range(4)]
            for z, b, d in geometry(slots, ry, i, base, pairs, cen):
                dens, pair, phi = pair_terms(vs[i, z, b])
                f = (sp + spairs[slots[z], base + b * (ry + 1), 0]) * dens + pair
                for c in range(3):
                    acc[c] = acc[c] + f * d[c]
                acc[3] = acc[3] + phi
            pick = slot_ref[r] == sub + (k * width + g * SUB).astype(jnp.float32)
            for c in range(4):
                part = jnp.sum(acc[c], axis=1, keepdims=True)
                values[r, c] = values[r, c] + jnp.where(pick, part, 0.0)
            return carry

        lax.fori_loop(STATIC, code >> 12, group, 0)
        return carry

    lax.fori_loop(0, 2 * tiles, rest, 0)

    for x in range(rx):
        for t in range(nt):
            r = x * nt + t
            for c in range(4):
                value = jnp.sum(values[r, c], axis=0, keepdims=True)
                if c < 3:
                    value = value * (4.0 / 3.0 * G2 / SCALE)
                else:
                    value = value * G2 - 1.0 - root_ref[r]
                value = jnp.where(slot_ref[r] >= 0.0, value, 0.0)
                for k in (0, 1):
                    part = value[:, k * half : (k + 1) * half]
                    if c < 3:
                        force_ref[c, 0, x, 2 * t + k : 2 * t + k + 1, :] = part
                    else:
                        energy_ref[0, x, 2 * t + k : 2 * t + k + 1, :] = part


def group_stride(half):
    return group_count(half)


def body(positions, counts):
    rx, ry, half = positions.shape[2:]
    nt, width = ry // 2, 2 * half
    f32 = jnp.float32
    sizes = tuple(lax.axis_size(axis) for axis in AXES)
    kept, slots = layer_slots(sizes[0])
    layers, tiles, cells = len(kept), rx * nt, rx * ry
    total = cells * group_stride(half)
    rows = (rx + 2) * (ry + 1)

    def vmem(*dims):
        return pltpu.VMEM(dims, f32)

    passed = (
            vmem(tiles, 1, width),
            vmem(tiles, 1, width),
            vmem(total, 3, SUB, width),
            vmem(layers, rows, 3, 1, width),
            vmem(total, LAYERS, 2, SUB, width),
            vmem(total, SUB, width),
            vmem(tiles, 1, width),
            vmem(layers, rows, 1, 1, width),
            vmem(total, 4, SUB, width),
    )
    held = sum(4 * math.prod(ref.shape) for ref in passed)
    shared = pl.pallas_call(
        functools.partial(step_kernel, sizes, rx, nt, half),
        out_shape=passed,
        in_specs=[HBM, HBM],
        out_specs=(VMEM,) * 9,
        scratch_shapes=[
            pltpu.SMEM(counts.shape, jnp.int32),
            vmem(*positions.shape),
            vmem(rx, nt, 3, 1, width),
            vmem(layers, rx + 2, nt + 2, 3, 1, width),
            vmem(3, tiles, width),
            vmem(tiles, 3, 1, width),
            pltpu.SMEM((total,), jnp.int32),
            vmem(total, SUB, width),
            vmem(rx, nt, 1, 1, width),
            vmem(layers, rx + 2, nt + 2, 1, 1, width),
            vmem(cells * STATIC, LAYERS, 2, 3, SUB, width),
            pltpu.SemaphoreType.DMA((2,)),
        ]
        + [pltpu.SemaphoreType.DMA((layers, 9))] * 4,
        compiler_params=pltpu.CompilerParams(
            collective_id=0, has_side_effects=True, vmem_limit_bytes=VMEM_BYTES - held - SPARE
        ),
        name="step",
    )(counts, positions)
    return pl.pallas_call(
        functools.partial(finish_kernel, slots, rx, nt, half),
        out_shape=(
            jax.ShapeDtypeStruct((3, 1, rx, ry, half), f32),
            jax.ShapeDtypeStruct((1, rx, ry, half), f32),
        ),
        in_specs=[VMEM] * 9,
        out_specs=(VMEM, VMEM),
        scratch_shapes=[pltpu.SMEM((cells,), jnp.int32), vmem(tiles, 4, SUB, width)],
        compiler_params=pltpu.CompilerParams(vmem_limit_bytes=24 * 2**20),
        name="finish",
    )(*shared)


def solution(mesh):
    return jax.shard_map(
        body,
        mesh=mesh,
        in_specs=(P(None, "gz", "gx", "gy", None), P("gz", "gx", "gy")),
        out_specs=(P(None, "gz", "gx", "gy", None), P("gz", "gx", "gy", None)),
        check_vma=False,
    )
```

profile of v0, /device:TPU:0, one launch (start us, length us, event | category | flops | bytes accessed | tf_op | source)
XLA Modules:
  0.0 27.8 jit_solution(7757881858446463447)
XLA Ops:
  0.6 24.7 %step.1 = (f32[8,1,128]{2,1,0:T(1,128)S(1)}, f32[8,1,128]{2,1,0:T(1,128)S(1)}, f32[176,3,8,128]{3,2,1,0:T(8,128)S(1)}, f32[4,36,3,1,128]{4,3,2,1,0:T(1,128)S(1)}...) custom-call(s32[1,2,8]{2,1,0:T(2,128)} %count_hbm.1, ...), custom_call_target="tpu_custom_call" | custom-call | tf_op jit(solution)/shard_map/step/pallas_call | solution.py:524
  25.3 2.5 %finish.1 = (f32[3,1,2,8,64]{4,3,2,1,0:T(8,128)}, f32[1,2,8,64]{3,2,1,0:T(8,128)}) custom-call(f32[8,1,128]{2,1,0:T(1,128)S(1)} %get-tuple-element.11.slot_ref, f32[8,1,128]{2,1,0:T(1,128)S(1)} %get-tuple-element.12.packed, f32[176,3,8,128]{3,2,1,0:T(8,128)S(1)} %get-tuple-element.13.cen, f32[4,36,3,1,128]{4,3,2,1,0:T(1,128)S(1)} %get-tuple-element.14.pairs, ...), custom_call_target="tpu_custom_call" | custom-call | tf_op jit(solution)/shard_map/finish/pallas_call | solution.py:549
where the time goes:
time: 27.9 us; the launch traced here: 27.8 us
  Pallas kernels  27.2 us (97%)
  between operations  0.64 us (2%)
    pallas_call x1, Pallas kernels, body(): pl.pallas_call(functools.partial(step_kernel, sizes, rx, nt, half), out_s...  24.7 us
    pallas_call x1, Pallas kernels, body(): pl.pallas_call(functools.partial(finish_kernel, slots, rx, nt, half), out...  2.5 us

commit v1 on v0

--- a/solution.py
+++ b/solution.py
@@ -109,7 +109,8 @@
 def start_copies(sizes, rx, nt, own, ext, send, recv):
     copies, _ = displacements(sizes)
     started = []
-    for s, b, c, step in copies:
+    far = {s: abs(a) for s, a in enumerate(layer_slots(sizes[0])[0])}
+    for s, b, c, step in sorted(copies, key=lambda copy: far[copy[0]]):
         copy = link(sizes, rx, nt, own, ext, send, recv, s, b, c, step)
         copy.start()
         if any(step):
@@ -117,8 +118,8 @@
     return started
 
 
-def wait_layer(sizes, rx, nt, own, ext, send, recv, slot, a):
-    for b in (-1, 0, 1):
+def wait_layer(sizes, rx, nt, own, ext, send, recv, slot, a, sides=(-1, 0, 1)):
+    for b in sides:
         for c in (-1, 0, 1):
             if a is None:
                 step = (1, 0, 0)
@@ -133,18 +134,22 @@
                 copy.wait()
 
 
+def offsets_of(nz, slot):
+    return [a for a in range(-DEPTH, DEPTH + 1) if layer_slots(nz)[1][a + DEPTH] == slot]
+
+
 def arrival_order(nz):
-    _, slots = layer_slots(nz)
+    kept, slots = layer_slots(nz)
+    home = slots[DEPTH]
     if nz < 4:
-        return [(slots[a + DEPTH], a, a + DEPTH, a) for a in (0, 1, -1, 2, -2)]
+        rest = [s for s in range(len(kept)) if s != home]
+        return [(s, kept[s], [(a, a + DEPTH) for a in offsets_of(nz, s)]) for s in [home] + rest]
     near = jnp.where(lax.axis_index("gz") == nz - 1, -1, 1)
-    return [
-        (slots[DEPTH], 0, DEPTH, 0),
-        (near + DEPTH, near, near + DEPTH, None),
-        (slots[0], -2, 0, -2),
-        (slots[2 * DEPTH], 2, 2 * DEPTH, 2),
-        (DEPTH - near, -near, DEPTH - near, None),
-    ]
+    order = [(home, 0, [(0, DEPTH)]), (near + DEPTH, None, [(near, near + DEPTH)])]
+    for s in sorted({slots[0], slots[2 * DEPTH]}):
+        order.append((s, kept[s], [(a, a + DEPTH) for a in offsets_of(nz, s)]))
+    order.append((DEPTH - near, None, [(-near, DEPTH - near)]))
+    return order
 
 
 def iota(shape, dim):
@@ -213,17 +218,17 @@
     return jnp.sum(jnp.where(lane == k * half, packed[r], 0.0)).astype(jnp.int32)
 
 
-def group_base(code, x, j, g, ry):
+def group_place(code, g):
     b1, b2, b3 = code & 15, (code >> 4) & 15, (code >> 8) & 15
     xhi = jnp.where(b2 <= g, 1, 0)
     yhi = jnp.where(b3 <= g, 1, jnp.where(b2 <= g, 0, jnp.where(b1 <= g, 1, 0)))
-    return (x + xhi) * (ry + 1) + j + yhi
+    return xhi, yhi
 
 
 def spread_centres(tiles, nt, ry, half, groups, stride, slot_ref, cent_row, packed, cen, meta):
     width = 2 * half
     sub = iota((SUB, width), 0).astype(jnp.float32)
-    upper = jnp.where(iota((SUB, width), 1) >= half, SLIDES[1], 0.0)
+    lean = jnp.where(iota((SUB, width), 1) >= half, 0.5 * SLIDES[1], -0.5 * SLIDES[1])
 
     def step(r, carry):
         slot = slot_ref[r]
@@ -233,20 +238,22 @@
             code = group_code(packed, r, k, half)
             for g in range(groups):
                 i = (2 * r + k) * stride + g
-                meta[i] = group_base(code, x, 2 * t + k, g, ry)
+                xhi, yhi = group_place(code, g)
+                meta[i] = (x + xhi) * (ry + 1) + 2 * t + k + yhi
+                sign = jnp.where(yhi == k, -1.0, 1.0)
                 pick = slot == sub + float(k * width + g * SUB)
                 for c in range(3):
                     column = jnp.sum(jnp.where(pick, rows[c], 0.0), axis=1, keepdims=True)
                     wide = jnp.broadcast_to(column, (SUB, width))
                     if c == 1:
-                        wide = wide - upper
+                        wide = wide - (0.5 * SLIDES[1] + sign * lean)
                     cen[i, c] = wide
         return carry
 
     lax.fori_loop(0, tiles, step, 0)
 
 
-def build_pairs(s, cols, ry, half, channels, ext, pairs):
+def build_pairs(s, first, last, ry, half, channels, ext, pairs):
     low = iota((1, 2 * half), 1) < half
 
     def step(x, carry):
@@ -256,33 +263,42 @@
                 if p % 2:
                     row = rows[(p + 1) // 2]
                 else:
-                    row = pltpu.roll(jnp.where(low, rows[p // 2 + 1], rows[p // 2]), half, 1)
+                    row = jnp.where(low, rows[p // 2 + 1], rows[p // 2])
                 pairs[s, x * (ry + 1) + p, c] = row
         return carry
 
-    lax.fori_loop(0, cols, step, 0, unroll=2)
-
-
-def density_layer(first, slot, shift, z, cells, groups, stride, ry, meta, pairs, cen, vs, rho):
-    def step(cell, carry):
-        for g in range(groups):
-            i = cell * stride + g
-            base = meta[i]
-            x, y, w = cen[i, 0], cen[i, 1], cen[i, 2]
-            if shift is not None:
-                w = w - shift
-            for b in (0, 1):
-                qx, qy, qz = (pairs[slot, base + b * (ry + 1), c] for c in range(3))
-                dx, dy, dz = x - qx, y - qy, w - qz
-                v = jnp.maximum(((REACH - dx * dx) - dy * dy) - dz * dz, 0.0)
-                vs[i, z, b] = v
-                part = jnp.exp2(v) * (v * v)
-                total = part if b == 0 else total + part
-                x = x - SLIDES[0]
-            rho[i] = total if first else rho[i] + total
-        return carry
-
-    lax.fori_loop(0, cells, step, 0, unroll=2)
+    lax.fori_loop(first, last, step, 0, unroll=2 if (last - first) % 2 == 0 else 1)
+
+
+def density_layer(
+    sides, first, slot, offsets, rx, groups, stride, ry, meta, pairs, cen, vs, rho
+):
+    def run(x_cell):
+        def step(j, carry):
+            for g in range(groups):
+                i = (x_cell * ry + j) * stride + g
+                base = meta[i]
+                x, y, w = cen[i, 0], cen[i, 1], cen[i, 2]
+                ws = [w if shift is None else w - shift for shift, _ in offsets]
+                total = None if first else rho[i]
+                for b in sides[x_cell]:
+                    qx, qy, qz = (pairs[slot, base + b * (ry + 1), c] for c in range(3))
+                    dx, dy = (x - SLIDES[0] if b else x) - qx, y - qy
+                    flat = (REACH - dx * dx) - dy * dy
+                    for wz, (_, z) in zip(ws, offsets):
+                        dz = wz - qz
+                        v = jnp.maximum(flat - dz * dz, 0.0)
+                        vs[i, z, b] = v
+                        part = jnp.exp2(v) * (v * v)
+                        total = part if total is None else total + part
+                rho[i] = jnp.zeros_like(x) if total is None else total
+            return carry
+
+        return step
+
+    for x_cell in range(rx):
+        if sides[x_cell] or first:
+            lax.fori_loop(0, ry, run(x_cell), 0, unroll=2)
 
 
 def slope_pass(tiles, nt, half, groups, stride, slot_ref, rho, cs, root_ref, sown, sext, home):
@@ -310,18 +326,7 @@
         sext[home, x + 1, t + 1, 0] = row
         return carry
 
-    lax.fori_loop(0, tiles, step, 0)
-
-
-def geometry(slots, ry, i, base, pairs, cen):
-    x, y, w = cen[i, 0], cen[i, 1], cen[i, 2]
-    for z in range(LAYERS):
-        a = z - DEPTH
-        wz = w - a * SLIDES[2] if a else w
-        for b in (0, 1):
-            q = [pairs[slots[z], base + b * (ry + 1), c] for c in range(3)]
-            xb = x - SLIDES[0] if b else x
-            yield z, b, (xb - q[0], y - q[1], wz - q[2])
+    lax.fori_loop(0, tiles, step, 0, unroll=4)
 
 
 def pair_terms(v):
@@ -330,17 +335,31 @@
     return g, w * (v + B), w * v
 
 
-def pair_pass(slots, cells, stride, ry, width, meta, pairs, cen, vs, gd, acc_ref):
+def pair_sums(nz, ry, i, base, pairs, cen, vs):
+    x, y, w = cen[i, 0], cen[i, 1], cen[i, 2]
+    ws = [w - a * SLIDES[2] if a else w for a in range(-DEPTH, DEPTH + 1)]
+    for slot in range(len(layer_slots(nz)[0])):
+        for b in (0, 1):
+            q = [pairs[slot, base + b * (ry + 1), c] for c in range(3)]
+            dx, dy = (x - SLIDES[0] if b else x) - q[0], y - q[1]
+            dens = pair = phi = dens_z = pair_z = 0.0
+            for a in offsets_of(nz, slot):
+                dz = ws[a + DEPTH] - q[2]
+                d, p, f = pair_terms(vs[i, a + DEPTH, b])
+                dens, pair, phi = dens + d, pair + p, phi + f
+                dens_z, pair_z = dens_z + d * dz, pair_z + p * dz
+            yield slot, b, (dens * dx, dens * dy, dens_z), (pair * dx, pair * dy, pair_z, phi)
+
+
+def pair_pass(nz, cells, stride, ry, width, meta, pairs, cen, vs, gd, acc_ref):
     def step(cell, carry):
         for g in range(STATIC):
             i = cell * stride + g
-            acc = [jnp.zeros((SUB, width), jnp.float32) for _ in range(4)]
-            for z, b, d in geometry(slots, ry, i, meta[i], pairs, cen):
-                dens, pair, phi = pair_terms(vs[i, z, b])
+            acc = [0.0] * 4
+            for slot, b, dens, pair in pair_sums(nz, ry, i, meta[i], pairs, cen, vs):
                 for c in range(3):
-                    gd[cell * STATIC + g, z, b, c] = dens * d[c]
-                    acc[c] = acc[c] + pair * d[c]
-                acc[3] = acc[3] + phi
+                    gd[cell * STATIC + g, slot, b, c] = dens[c]
+                acc = [total + part for total, part in zip(acc, pair)]
             for c in range(4):
                 acc_ref[i, c] = acc[c]
         return carry
@@ -354,11 +373,11 @@
             i = cell * stride + g
             base, sp = meta[i], cs[i]
             acc = [acc_ref[i, c] for c in range(3)]
-            for slot, z in layers:
+            for slot in layers:
                 for b in (0, 1):
                     f = sp + spairs[slot, base + b * (ry + 1), 0]
                     for c in range(3):
-                        acc[c] = acc[c] + f * gd[cell * STATIC + g, z, b, c]
+                        acc[c] = acc[c] + f * gd[cell * STATIC + g, slot, b, c]
             for c in range(3):
                 acc_ref[i, c] = acc[c]
         return carry
@@ -388,42 +407,56 @@
     for copy in loads:
         copy.wait()
     load_rows(rx, nt, half, home, count_ref, pos_ref, own, ext, raw)
+    assign_slots(tiles, half, raw, slot_ref, cent_row, packed)
+    spread_centres(tiles, nt, ry, half, groups, stride, slot_ref, cent_row, packed, cen, meta)
     pl.semaphore_wait(barrier, arrivals)
     sends = start_copies(sizes, rx, nt, own, ext, send, recv)
-    assign_slots(tiles, half, raw, slot_ref, cent_row, packed)
-    spread_centres(tiles, nt, ry, half, groups, stride, slot_ref, cent_row, packed, cen, meta)
 
     def arrive(e, own_ref, ext_ref, send_sem, recv_sem, channels, pairs_ref):
-        slot, _, _, known = order[e]
-        seen = [o[0] for o in order[:e] if isinstance(o[0], int)]
-        if isinstance(slot, int) and slot in seen:
-            return
+        slot, known, _ = order[e]
         wait_layer(sizes, rx, nt, own_ref, ext_ref, send_sem, recv_sem, slot, known)
-        build_pairs(slot, rx + 2, ry, half, channels, ext_ref, pairs_ref)
-
-    for e, (slot, a, z, known) in enumerate(order):
+        build_pairs(slot, 0, rx + 2, ry, half, channels, ext_ref, pairs_ref)
+
+    def density(sides, first, e):
+        slot, known, offsets = order[e]
+        shifted = []
+        for a, z in offsets:
+            if known is None:
+                shifted.append((a.astype(jnp.float32) * SLIDES[2], z))
+            else:
+                shifted.append((a * SLIDES[2] if a else None, z))
+        density_layer(
+            sides, first, slot, shifted, rx, groups, stride, ry, meta, pairs, cen, vs, rho
+        )
+
+    both = [(0, 1)] * rx
+    inner = [tuple(b for b in (0, 1) if 1 <= x + b and x + b < rx) for x in range(rx)]
+    outer = [tuple(b for b in (0, 1) if b not in inner[x]) for x in range(rx)]
+    wait_layer(sizes, rx, nt, own, ext, send, recv, home, 0, (0,))
+    build_pairs(home, 1, rx + 1, ry, half, 3, ext, pairs)
+    density(inner, True, 0)
+    wait_layer(sizes, rx, nt, own, ext, send, recv, home, 0, (-1, 1))
+    build_pairs(home, 0, 1, ry, half, 3, ext, pairs)
+    build_pairs(home, rx + 1, rx + 2, ry, half, 3, ext, pairs)
+    density(outer, False, 0)
+    for e in range(1, len(order)):
         arrive(e, own, ext, send, recv, 3, pairs)
-        if known is None:
-            shift = a.astype(jnp.float32) * SLIDES[2]
-        else:
-            shift = known * SLIDES[2] if known else None
-        density_layer(
-            e == 0, slot, shift, z, cells, groups, stride, ry, meta, pairs, cen, vs, rho
-        )
+        density(both, False, e)
     slope_pass(tiles, nt, half, groups, stride, slot_ref, rho, cs, root_ref, sown, sext, home)
     sends += start_copies(sizes, rx, nt, sown, sext, send2, recv2)
-    pair_pass(slots, cells, stride, ry, width, meta, pairs, cen, vs, gd, acc_ref)
-    for chunk in ((0, 1), (2, 3), (4,)):
+    pair_pass(sizes[0], cells, stride, ry, width, meta, pairs, cen, vs, gd, acc_ref)
+    for chunk in [(0, 1)] + [(e,) for e in range(2, len(order))]:
+        chunk = [e for e in chunk if e < len(order)]
         for e in chunk:
             arrive(e, sown, sext, send2, recv2, 1, spairs)
-        layers = [(order[e][0], order[e][2]) for e in chunk]
+        layers = [order[e][0] for e in chunk]
         slope_force(layers, cells, stride, ry, meta, spairs, cs, gd, acc_ref)
     for copy in sends:
         copy.wait_send()
 
 
 def finish_kernel(
-    slots, rx, nt, half, slot_ref, packed, cen, pairs, vs, cs, root_ref, spairs, acc_ref,
+    nz, rx, nt, half, slot_ref, packed, cen, pairs, vs, cs, root_ref, spairs, acc_ref,
     force_ref, energy_ref, codes, values,
 ):
     width, ry, tiles = 2 * half, 2 * nt, rx * nt
@@ -455,14 +488,15 @@
 
         def group(g, carry):
             i = cell * stride + g
-            base, sp = group_base(code, x, j, g, ry), cs[i]
-            acc = [jnp.zeros((SUB, width), jnp.float32) for _ in range(4)]
-            for z, b, d in geometry(slots, ry, i, base, pairs, cen):
-                dens, pair, phi = pair_terms(vs[i, z, b])
-                f = (sp + spairs[slots[z], base + b * (ry + 1), 0]) * dens + pair
+            sp = cs[i]
+            xhi, yhi = group_place(code, g)
+            base = (x + xhi) * (ry + 1) + j + yhi
+            acc = [0.0] * 4
+            for slot, b, dens, pair in pair_sums(nz, ry, i, base, pairs, cen, vs):
+                f = sp + spairs[slot, base + b * (ry + 1), 0]
                 for c in range(3):
-                    acc[c] = acc[c] + f * d[c]
-                acc[3] = acc[3] + phi
+                    acc[c] = acc[c] + f * dens[c] + pair[c]
+                acc[3] = acc[3] + pair[3]
             pick = slot_ref[r] == sub + (k * width + g * SUB).astype(jnp.float32)
             for c in range(4):
                 part = jnp.sum(acc[c], axis=1, keepdims=True)
@@ -501,7 +535,7 @@
     nt, width = ry // 2, 2 * half
     f32 = jnp.float32
     sizes = tuple(lax.axis_size(axis) for axis in AXES)
-    kept, slots = layer_slots(sizes[0])
+    kept, _ = layer_slots(sizes[0])
     layers, tiles, cells = len(kept), rx * nt, rx * ry
     total = cells * group_stride(half)
     rows = (rx + 2) * (ry + 1)
@@ -537,7 +571,7 @@
             vmem(total, SUB, width),
             vmem(rx, nt, 1, 1, width),
             vmem(layers, rx + 2, nt + 2, 1, 1, width),
-            vmem(cells * STATIC, LAYERS, 2, 3, SUB, width),
+            vmem(cells * STATIC, layers, 2, 3, SUB, width),
             pltpu.SemaphoreType.DMA((2,)),
         ]
         + [pltpu.SemaphoreType.DMA((layers, 9))] * 4,
@@ -547,7 +581,7 @@
         name="step",
     )(counts, positions)
     return pl.pallas_call(
-        functools.partial(finish_kernel, slots, rx, nt, half),
+        functools.partial(finish_kernel, sizes[0], rx, nt, half),
         out_shape=(
             jax.ShapeDtypeStruct((3, 1, rx, ry, half), f32),
             jax.ShapeDtypeStruct((1, rx, ry, half), f32),

time: 27.9 us -> 25.1 us (0.90)
  Pallas kernels: 27.2 us -> 24.4 us
    pallas_call x1, Pallas kernels: 24.7 us -> 22 us  [body(): pl.pallas_call(functools.partial(step_kernel, sizes, rx, nt, half), out_s...]
where the time goes in v1:
time: 25.1 us; the launch traced here: 25 us
  Pallas kernels  24.4 us (97%)
  between operations  0.64 us (3%)
    pallas_call x1, Pallas kernels, body(): pl.pallas_call(functools.partial(step_kernel, sizes, rx, nt, half), out_s...  22 us
    pallas_call x1, Pallas kernels, body(): pl.pallas_call(functools.partial(finish_kernel, sizes[0], rx, nt, half),...  2.41 us

profile of v1, /device:TPU:0, one launch (start us, length us, event | category | flops | bytes accessed | tf_op | source)
XLA Modules:
  0.0 25.0 jit_solution(11833234259453602535)
XLA Ops:
  0.6 22.0 %step.1 = (f32[8,1,128]{2,1,0:T(1,128)S(1)}, f32[8,1,128]{2,1,0:T(1,128)S(1)}, f32[176,3,8,128]{3,2,1,0:T(8,128)S(1)}, f32[4,36,3,1,128]{4,3,2,1,0:T(1,128)S(1)}...) custom-call(s32[1,2,8]{2,1,0:T(2,128)} %count_hbm.1, ...), custom_call_target="tpu_custom_call" | custom-call | tf_op jit(solution)/shard_map/step/pallas_call | solution.py:558
  22.6 2.4 %finish.1 = (f32[3,1,2,8,64]{4,3,2,1,0:T(8,128)}, f32[1,2,8,64]{3,2,1,0:T(8,128)}) custom-call(f32[8,1,128]{2,1,0:T(1,128)S(1)} %get-tuple-element.11.slot_ref, f32[8,1,128]{2,1,0:T(1,128)S(1)} %get-tuple-element.12.packed, f32[176,3,8,128]{3,2,1,0:T(8,128)S(1)} %get-tuple-element.13.cen, f32[4,36,3,1,128]{4,3,2,1,0:T(1,128)S(1)} %get-tuple-element.14.pairs, ...), custom_call_target="tpu_custom_call" | custom-call | tf_op jit(solution)/shard_map/finish/pallas_call | solution.py:583

commit v2 on v1

--- a/solution.py
+++ b/solution.py
@@ -64,7 +64,7 @@
 
 def device(step, sizes):
     return {
-        axis: lax.rem(lax.axis_index(axis) + d, n)
+        axis: lax.rem(lax.axis_index(axis) + d + n, n)
         for axis, d, n in zip(AXES, step, sizes)
     }
 
@@ -90,48 +90,83 @@
     return pl.ds(0, 1), pl.ds(length + 1, 1)
 
 
-def link(sizes, rx, nt, own, ext, send, recv, s, b, c, step):
+def link(sizes, rx, nt, own, ext, send, recv, slot, b, c, step):
     (sx, dx), (st, dt) = edge(b, rx), edge(c, nt)
-    source, target = own.at[sx, st], ext.at[s, dx, dt]
+    source, target = own.at[sx, st], ext.at[slot, dx, dt]
     j = 3 * (b + 1) + c + 1
-    if not any(step):
-        return pltpu.make_async_copy(source, target, recv.at[s, j])
+    if step is None:
+        return pltpu.make_async_copy(source, target, recv.at[slot, j])
     return pltpu.make_async_remote_copy(
         src_ref=source,
         dst_ref=target,
-        send_sem=send.at[s, j],
-        recv_sem=recv.at[s, j],
+        send_sem=send.at[slot, j],
+        recv_sem=recv.at[slot, j],
         device_id=device(step, sizes),
         device_id_type=pl.DeviceIdType.MESH,
     )
 
 
-def start_copies(sizes, rx, nt, own, ext, send, recv):
-    copies, _ = displacements(sizes)
-    started = []
-    far = {s: abs(a) for s, a in enumerate(layer_slots(sizes[0])[0])}
-    for s, b, c, step in sorted(copies, key=lambda copy: far[copy[0]]):
-        copy = link(sizes, rx, nt, own, ext, send, recv, s, b, c, step)
-        copy.start()
-        if any(step):
-            started.append(copy)
-    return started
-
-
-def wait_layer(sizes, rx, nt, own, ext, send, recv, slot, a, sides=(-1, 0, 1)):
+def layer_links(sizes, rx, nt, own, ext, send, recv, slot, dz, sides=(-1, 0, 1)):
+    found = []
     for b in sides:
         for c in (-1, 0, 1):
-            if a is None:
-                step = (1, 0, 0)
-            else:
-                if (a, b, c) == (0, 0, 0):
+            step = (dz, -b, -c)
+            if isinstance(dz, int):
+                step = tuple(d % n for d, n in zip(step, sizes))
+                if (dz, b, c) == (0, 0, 0):
                     continue
-                step = tuple(-o % n for o, n in zip((a, b, c), sizes))
+                if not any(step):
+                    step = None
             copy = link(sizes, rx, nt, own, ext, send, recv, slot, b, c, step)
-            if any(step):
-                copy.wait_recv()
-            else:
-                copy.wait()
+            found.append((copy, step is not None))
+    return found
+
+
+def start_layer(*where):
+    for copy, _ in layer_links(*where):
+        copy.start()
+
+
+def wait_layer(*where):
+    for copy, remote in layer_links(*where):
+        if remote:
+            copy.wait_recv()
+        else:
+            copy.wait()
+
+
+def start_copies(sizes, rx, nt, own, ext, send, recv):
+    nz = sizes[0]
+    place = (sizes, rx, nt, own, ext, send, recv)
+    kept, slots = layer_slots(nz)
+    start_layer(*place, slots[DEPTH], 0)
+    if nz < 4:
+        for slot, a in enumerate(kept):
+            if a:
+                start_layer(*place, slot, -a)
+        return
+    near, middle = nearest(nz)
+
+    def start_far():
+        start_layer(*place, DEPTH + near, -near)
+
+    start_layer(*place, DEPTH - near, near)
+    pl.when(middle)(start_far)
+    for slot in sorted({slots[0], slots[2 * DEPTH]}):
+        start_layer(*place, slot, -kept[slot])
+    pl.when(jnp.logical_not(middle))(start_far)
+
+
+def wait_sends(sizes, rx, nt, own, ext, send, recv):
+    for slot, a in enumerate(layer_slots(sizes[0])[0]):
+        for copy, remote in layer_links(sizes, rx, nt, own, ext, send, recv, slot, -a):
+            if remote:
+                copy.wait_send()
+
+
+def nearest(nz):
+    z = lax.axis_index("gz")
+    return jnp.where(lax.rem(z, 2) == 0, 1, -1), (z != 0) & (z != nz - 1)
 
 
 def offsets_of(nz, slot):
@@ -144,7 +179,7 @@
     if nz < 4:
         rest = [s for s in range(len(kept)) if s != home]
         return [(s, kept[s], [(a, a + DEPTH) for a in offsets_of(nz, s)]) for s in [home] + rest]
-    near = jnp.where(lax.axis_index("gz") == nz - 1, -1, 1)
+    near, _ = nearest(nz)
     order = [(home, 0, [(0, DEPTH)]), (near + DEPTH, None, [(near, near + DEPTH)])]
     for s in sorted({slots[0], slots[2 * DEPTH]}):
         order.append((s, kept[s], [(a, a + DEPTH) for a in offsets_of(nz, s)]))
@@ -225,7 +260,7 @@
     return xhi, yhi
 
 
-def spread_centres(tiles, nt, ry, half, groups, stride, slot_ref, cent_row, packed, cen, meta):
+def spread_centres(tiles, nt, ry, half, groups, stride, slot_ref, cent_row, packed, cen, dens, meta):
     width = 2 * half
     sub = iota((SUB, width), 0).astype(jnp.float32)
     lean = jnp.where(iota((SUB, width), 1) >= half, 0.5 * SLIDES[1], -0.5 * SLIDES[1])
@@ -242,52 +277,76 @@
                 meta[i] = (x + xhi) * (ry + 1) + 2 * t + k + yhi
                 sign = jnp.where(yhi == k, -1.0, 1.0)
                 pick = slot == sub + float(k * width + g * SUB)
+                p = []
                 for c in range(3):
                     column = jnp.sum(jnp.where(pick, rows[c], 0.0), axis=1, keepdims=True)
                     wide = jnp.broadcast_to(column, (SUB, width))
                     if c == 1:
                         wide = wide - (0.5 * SLIDES[1] + sign * lean)
                     cen[i, c] = wide
+                    dens[i, c] = wide + wide
+                    p.append(wide)
+                flat = (REACH - p[1] * p[1]) - p[2] * p[2]
+                next_x = p[0] - SLIDES[0]
+                dens[i, 3] = flat - p[0] * p[0]
+                dens[i, 4] = flat - next_x * next_x
         return carry
 
-    lax.fori_loop(0, tiles, step, 0)
-
-
-def build_pairs(s, first, last, ry, half, channels, ext, pairs):
+    lax.fori_loop(0, tiles, step, 0, unroll=2)
+
+
+def pair_row(rows, p, half):
+    if p % 2:
+        return rows[(p + 1) // 2]
     low = iota((1, 2 * half), 1) < half
-
+    return jnp.where(low, rows[p // 2 + 1], rows[p // 2])
+
+
+def build_pairs(s, first, last, ry, half, shifts, ext, pairs):
     def step(x, carry):
-        for c in range(channels):
-            rows = [ext[s, x, t, c] for t in range(ry // 2 + 2)]
-            for p in range(ry + 1):
-                if p % 2:
-                    row = rows[(p + 1) // 2]
-                else:
-                    row = jnp.where(low, rows[p // 2 + 1], rows[p // 2])
-                pairs[s, x * (ry + 1) + p, c] = row
+        rows = [[ext[s, x, t, c] for t in range(ry // 2 + 2)] for c in range(3)]
+        for p in range(ry + 1):
+            at = x * (ry + 1) + p
+            qx, qy, qz = (pair_row(rows[c], p, half) for c in range(3))
+            pairs[s, at, 0], pairs[s, at, 1] = qx, qy
+            flat = qx * qx + qy * qy
+            for k, shift in enumerate(shifts):
+                q = qz if shift is None else qz + shift
+                pairs[s, at, 2 + 2 * k] = q
+                pairs[s, at, 3 + 2 * k] = -(flat + q * q)
         return carry
 
     lax.fori_loop(first, last, step, 0, unroll=2 if (last - first) % 2 == 0 else 1)
 
 
+def build_slopes(s, cols, ry, half, ext, pairs):
+    def step(x, carry):
+        rows = [ext[s, x, t, 0] for t in range(ry // 2 + 2)]
+        for p in range(ry + 1):
+            pairs[s, x * (ry + 1) + p, 0] = pair_row(rows, p, half)
+        return carry
+
+    lax.fori_loop(0, cols, step, 0, unroll=2)
+
+
 def density_layer(
-    sides, first, slot, offsets, rx, groups, stride, ry, meta, pairs, cen, vs, rho
+    sides, first, slot, offsets, rx, groups, stride, ry, meta, pairs, table, vs, rho
 ):
     def run(x_cell):
         def step(j, carry):
             for g in range(groups):
                 i = (x_cell * ry + j) * stride + g
                 base = meta[i]
-                x, y, w = cen[i, 0], cen[i, 1], cen[i, 2]
-                ws = [w if shift is None else w - shift for shift, _ in offsets]
+                x, y, w = table[i, 0], table[i, 1], table[i, 2]
                 total = None if first else rho[i]
                 for b in sides[x_cell]:
-                    qx, qy, qz = (pairs[slot, base + b * (ry + 1), c] for c in range(3))
-                    dx, dy = (x - SLIDES[0] if b else x) - qx, y - qy
-                    flat = (REACH - dx * dx) - dy * dy
-                    for wz, (_, z) in zip(ws, offsets):
-                        dz = wz - qz
-                        v = jnp.maximum(flat - dz * dz, 0.0)
+                    at = base + b * (ry + 1)
+                    qx, qy = pairs[slot, at, 0], pairs[slot, at, 1]
+                    xb = x - 2.0 * SLIDES[0] if b else x
+                    flat = (table[i, 3 + b] + xb * qx) + y * qy
+                    for k, z in enumerate(offsets):
+                        qz, cq = pairs[slot, at, 2 + 2 * k], pairs[slot, at, 3 + 2 * k]
+                        v = jnp.maximum(flat + (cq + w * qz), 0.0)
                         vs[i, z, b] = v
                         part = jnp.exp2(v) * (v * v)
                         total = part if total is None else total + part
@@ -335,36 +394,47 @@
     return g, w * (v + B), w * v
 
 
-def pair_sums(nz, ry, i, base, pairs, cen, vs):
+def pair_sums(nz, spots, ry, i, base, pairs, cen, vs):
     x, y, w = cen[i, 0], cen[i, 1], cen[i, 2]
-    ws = [w - a * SLIDES[2] if a else w for a in range(-DEPTH, DEPTH + 1)]
-    for slot in range(len(layer_slots(nz)[0])):
-        for b in (0, 1):
-            q = [pairs[slot, base + b * (ry + 1), c] for c in range(3)]
-            dx, dy = (x - SLIDES[0] if b else x) - q[0], y - q[1]
-            dens = pair = phi = dens_z = pair_z = 0.0
-            for a in offsets_of(nz, slot):
-                dz = ws[a + DEPTH] - q[2]
-                d, p, f = pair_terms(vs[i, a + DEPTH, b])
-                dens, pair, phi = dens + d, pair + p, phi + f
-                dens_z, pair_z = dens_z + d * dz, pair_z + p * dz
-            yield slot, b, (dens * dx, dens * dy, dens_z), (pair * dx, pair * dy, pair_z, phi)
-
-
-def pair_pass(nz, cells, stride, ry, width, meta, pairs, cen, vs, gd, acc_ref):
-    def step(cell, carry):
-        for g in range(STATIC):
-            i = cell * stride + g
-            acc = [0.0] * 4
-            for slot, b, dens, pair in pair_sums(nz, ry, i, meta[i], pairs, cen, vs):
-                for c in range(3):
-                    gd[cell * STATIC + g, slot, b, c] = dens[c]
-                acc = [total + part for total, part in zip(acc, pair)]
-            for c in range(4):
-                acc_ref[i, c] = acc[c]
-        return carry
-
-    lax.fori_loop(0, cells, step, 0)
+    for slot, b in spots:
+        at = base + b * (ry + 1)
+        dx = (x - SLIDES[0] if b else x) - pairs[slot, at, 0]
+        dy = y - pairs[slot, at, 1]
+        dens = pair = phi = dens_z = pair_z = 0.0
+        for k, a in enumerate(offsets_of(nz, slot)):
+            dz = w - pairs[slot, at, 2 + 2 * k]
+            d, p, f = pair_terms(vs[i, a + DEPTH, b])
+            dens, pair, phi = dens + d, pair + p, phi + f
+            dens_z, pair_z = dens_z + d * dz, pair_z + p * dz
+        yield slot, b, (dens * dx, dens * dy, dens_z), (pair * dx, pair * dy, pair_z, phi)
+
+
+def pair_pass(
+    nz, spots, first, rx, stride, ry, width, meta, pairs, cen, vs, gd, acc_ref
+):
+    def run(x_cell):
+        def step(j, carry):
+            cell = x_cell * ry + j
+            for g in range(STATIC):
+                i = cell * stride + g
+                if first:
+                    acc = [jnp.zeros((SUB, width), jnp.float32)] * 4
+                else:
+                    acc = [acc_ref[i, c] for c in range(4)]
+                sums = pair_sums(nz, spots[x_cell], ry, i, meta[i], pairs, cen, vs)
+                for slot, b, dens, pair in sums:
+                    for c in range(3):
+                        gd[cell * STATIC + g, slot, b, c] = dens[c]
+                    acc = [total + part for total, part in zip(acc, pair)]
+                for c in range(4):
+                    acc_ref[i, c] = acc[c]
+            return carry
+
+        return step
+
+    for x_cell in range(rx):
+        if spots[x_cell] or first:
+            lax.fori_loop(0, ry, run(x_cell), 0)
 
 
 def slope_force(layers, cells, stride, ry, meta, spairs, cs, gd, acc_ref):
@@ -387,8 +457,7 @@
 
 def step_kernel(
     sizes, rx, nt, half, count_hbm, pos_hbm, slot_ref, packed, cen, pairs, vs, cs, root_ref,
-    spairs, acc_ref, count_ref, pos_ref, own, ext, raw, cent_row, meta, rho, sown, sext, gd,
-    load, send, recv, send2, recv2,
+    spairs, acc_ref, count_ref, pos_ref, own, ext, raw, cent_row, meta, rho, sown, sext, gd, table, load, send, recv, send2, recv2,
 ):
     loads = [
         pltpu.make_async_copy(count_hbm, count_ref, load.at[0]),
@@ -408,51 +477,80 @@
         copy.wait()
     load_rows(rx, nt, half, home, count_ref, pos_ref, own, ext, raw)
     assign_slots(tiles, half, raw, slot_ref, cent_row, packed)
-    spread_centres(tiles, nt, ry, half, groups, stride, slot_ref, cent_row, packed, cen, meta)
+    spread_centres(tiles, nt, ry, half, groups, stride, slot_ref, cent_row, packed, cen, table, meta)
     pl.semaphore_wait(barrier, arrivals)
-    sends = start_copies(sizes, rx, nt, own, ext, send, recv)
-
-    def arrive(e, own_ref, ext_ref, send_sem, recv_sem, channels, pairs_ref):
+    where = (sizes, rx, nt, own, ext, send, recv)
+    swhere = (sizes, rx, nt, sown, sext, send2, recv2)
+    start_copies(*where)
+
+    def arrive(e, place):
         slot, known, _ = order[e]
-        wait_layer(sizes, rx, nt, own_ref, ext_ref, send_sem, recv_sem, slot, known)
-        build_pairs(slot, 0, rx + 2, ry, half, channels, ext_ref, pairs_ref)
+        wait_layer(*place, slot, 1 if known is None else -known)
+
+    def shifts_of(e):
+        _, known, offsets = order[e]
+        if known is None:
+            return [offsets[0][0].astype(jnp.float32) * SLIDES[2]]
+        return [a * SLIDES[2] if a else None for a, _ in offsets]
 
     def density(sides, first, e):
-        slot, known, offsets = order[e]
-        shifted = []
-        for a, z in offsets:
-            if known is None:
-                shifted.append((a.astype(jnp.float32) * SLIDES[2], z))
-            else:
-                shifted.append((a * SLIDES[2] if a else None, z))
+        slot, _, offsets = order[e]
+        zs = [z for _, z in offsets]
         density_layer(
-            sides, first, slot, shifted, rx, groups, stride, ry, meta, pairs, cen, vs, rho
+            sides, first, slot, zs, rx, groups, stride, ry, meta, pairs, table, vs, rho
         )
+
+    def pairwise(spots, first):
+        pair_pass(
+            sizes[0], spots, first, rx, stride, ry, width, meta, pairs, cen, vs, gd, acc_ref
+        )
+
+    def pair_home(sides, first):
+        pairwise([[(home, b) for b in side] for side in sides], first)
 
     both = [(0, 1)] * rx
     inner = [tuple(b for b in (0, 1) if 1 <= x + b and x + b < rx) for x in range(rx)]
     outer = [tuple(b for b in (0, 1) if b not in inner[x]) for x in range(rx)]
-    wait_layer(sizes, rx, nt, own, ext, send, recv, home, 0, (0,))
-    build_pairs(home, 1, rx + 1, ry, half, 3, ext, pairs)
+    wait_layer(*where, home, 0, (0,))
+    build_pairs(home, 1, rx + 1, ry, half, [None], ext, pairs)
     density(inner, True, 0)
-    wait_layer(sizes, rx, nt, own, ext, send, recv, home, 0, (-1, 1))
-    build_pairs(home, 0, 1, ry, half, 3, ext, pairs)
-    build_pairs(home, rx + 1, rx + 2, ry, half, 3, ext, pairs)
+    wait_layer(*where, home, 0, (-1, 1))
+    build_pairs(home, 0, 1, ry, half, [None], ext, pairs)
+    build_pairs(home, rx + 1, rx + 2, ry, half, [None], ext, pairs)
     density(outer, False, 0)
-    for e in range(1, len(order)):
-        arrive(e, own, ext, send, recv, 3, pairs)
+    pair_home(inner, True)
+
+    def take(e):
+        arrive(e, where)
+        build_pairs(order[e][0], 0, rx + 2, ry, half, shifts_of(e), ext, pairs)
         density(both, False, e)
+
+    last = len(order) - 1
+    if sizes[0] < 4:
+        for e in range(1, len(order)):
+            take(e)
+        pair_home(outer, False)
+    else:
+        _, middle = nearest(sizes[0])
+        take(1)
+        pl.when(middle)(lambda: take(last))
+        for e in range(2, last):
+            take(e)
+        pl.when(jnp.logical_not(middle))(lambda: take(last))
     slope_pass(tiles, nt, half, groups, stride, slot_ref, rho, cs, root_ref, sown, sext, home)
-    sends += start_copies(sizes, rx, nt, sown, sext, send2, recv2)
-    pair_pass(sizes[0], cells, stride, ry, width, meta, pairs, cen, vs, gd, acc_ref)
+    start_copies(*swhere)
+    pair_home(outer, False)
+    away = [(s, b) for s in range(len(kept)) if s != home for b in (0, 1)]
+    pairwise([away] * rx, False)
     for chunk in [(0, 1)] + [(e,) for e in range(2, len(order))]:
         chunk = [e for e in chunk if e < len(order)]
         for e in chunk:
-            arrive(e, sown, sext, send2, recv2, 1, spairs)
+            arrive(e, swhere)
+            build_slopes(order[e][0], rx + 2, ry, half, sext, spairs)
         layers = [order[e][0] for e in chunk]
         slope_force(layers, cells, stride, ry, meta, spairs, cs, gd, acc_ref)
-    for copy in sends:
-        copy.wait_send()
+    wait_sends(*where)
+    wait_sends(*swhere)
 
 
 def finish_kernel(
@@ -462,6 +560,7 @@
     width, ry, tiles = 2 * half, 2 * nt, rx * nt
     stride = group_stride(half)
     sub = iota((SUB, width), 0).astype(jnp.float32)
+    spots = [(s, b) for s in range(len(layer_slots(nz)[0])) for b in (0, 1)]
     for r in range(tiles):
         for k in (0, 1):
             codes[2 * r + k] = group_code(packed, r, k, half)
@@ -479,7 +578,7 @@
             values[r, c] = total[c]
         return carry
 
-    lax.fori_loop(0, tiles, gather, 0, unroll=2)
+    lax.fori_loop(0, tiles, gather, 0, unroll=4)
 
     def rest(cell, carry):
         r, k = cell // 2, cell % 2
@@ -492,7 +591,7 @@
             xhi, yhi = group_place(code, g)
             base = (x + xhi) * (ry + 1) + j + yhi
             acc = [0.0] * 4
-            for slot, b, dens, pair in pair_sums(nz, ry, i, base, pairs, cen, vs):
+            for slot, b, dens, pair in pair_sums(nz, spots, ry, i, base, pairs, cen, vs):
                 f = sp + spairs[slot, base + b * (ry + 1), 0]
                 for c in range(3):
                     acc[c] = acc[c] + f * dens[c] + pair[c]
@@ -539,6 +638,7 @@
     layers, tiles, cells = len(kept), rx * nt, rx * ry
     total = cells * group_stride(half)
     rows = (rx + 2) * (ry + 1)
+    channels = 2 + 2 * max(len(offsets_of(sizes[0], s)) for s in range(layers))
 
     def vmem(*dims):
         return pltpu.VMEM(dims, f32)
@@ -547,7 +647,7 @@
             vmem(tiles, 1, width),
             vmem(tiles, 1, width),
             vmem(total, 3, SUB, width),
-            vmem(layers, rows, 3, 1, width),
+            vmem(layers, rows, channels, 1, width),
             vmem(total, LAYERS, 2, SUB, width),
             vmem(total, SUB, width),
             vmem(tiles, 1, width),
@@ -559,7 +659,7 @@
         functools.partial(step_kernel, sizes, rx, nt, half),
         out_shape=passed,
         in_specs=[HBM, HBM],
-        out_specs=(VMEM,) * 9,
+        out_specs=(VMEM,) * len(passed),
         scratch_shapes=[
             pltpu.SMEM(counts.shape, jnp.int32),
             vmem(*positions.shape),
@@ -572,6 +672,7 @@
             vmem(rx, nt, 1, 1, width),
             vmem(layers, rx + 2, nt + 2, 1, 1, width),
             vmem(cells * STATIC, layers, 2, 3, SUB, width),
+            vmem(total, 5, SUB, width),
             pltpu.SemaphoreType.DMA((2,)),
         ]
         + [pltpu.SemaphoreType.DMA((layers, 9))] * 4,
@@ -586,7 +687,7 @@
             jax.ShapeDtypeStruct((3, 1, rx, ry, half), f32),
             jax.ShapeDtypeStruct((1, rx, ry, half), f32),
         ),
-        in_specs=[VMEM] * 9,
+        in_specs=[VMEM] * len(passed),
         out_specs=(VMEM, VMEM),
         scratch_shapes=[pltpu.SMEM((cells,), jnp.int32), vmem(tiles, 4, SUB, width)],
         compiler_params=pltpu.CompilerParams(vmem_limit_bytes=24 * 2**20),

time: 25.1 us -> 24.6 us (0.980)
  Pallas kernels: 24.4 us -> 23.8 us
    pallas_call x1, Pallas kernels: 22 us -> 21.6 us  [body(): pl.pallas_call(functools.partial(step_kernel, sizes, rx, nt, half), out_s...]
where the time goes in v2:
time: 24.6 us; the launch traced here: 24.5 us
  Pallas kernels  23.8 us (97%)
  between operations  0.64 us (3%)
    pallas_call x1, Pallas kernels, body(): pl.pallas_call(functools.partial(step_kernel, sizes, rx, nt, half), out_s...  21.6 us
    pallas_call x1, Pallas kernels, body(): pl.pallas_call(functools.partial(finish_kernel, sizes[0], rx, nt, half),...  2.27 us

profile of v2, /device:TPU:0, one launch (start us, length us, event | category | flops | bytes accessed | tf_op | source)
XLA Modules:
  0.0 24.5 jit_solution(261961029360783483)
XLA Ops:
  0.6 21.6 %step.1 = (f32[8,1,128]{2,1,0:T(1,128)S(1)}, f32[8,1,128]{2,1,0:T(1,128)S(1)}, f32[176,3,8,128]{3,2,1,0:T(8,128)S(1)}, f32[4,36,6,1,128]{4,3,2,1,0:T(1,128)S(1)}...) custom-call(s32[1,2,8]{2,1,0:T(2,128)} %count_hbm.1, ...), custom_call_target="tpu_custom_call" | custom-call | tf_op jit(solution)/shard_map/step/pallas_call | solution.py:658
  22.2 2.3 %finish.1 = (f32[3,1,2,8,64]{4,3,2,1,0:T(8,128)}, f32[1,2,8,64]{3,2,1,0:T(8,128)}) custom-call(f32[8,1,128]{2,1,0:T(1,128)S(1)} %get-tuple-element.11.slot_ref, f32[8,1,128]{2,1,0:T(1,128)S(1)} %get-tuple-element.12.packed, f32[176,3,8,128]{3,2,1,0:T(8,128)S(1)} %get-tuple-element.13.cen, f32[4,36,6,1,128]{4,3,2,1,0:T(1,128)S(1)} %get-tuple-element.14.pairs, ...), custom_call_target="tpu_custom_call" | custom-call | tf_op jit(solution)/shard_map/finish/pallas_call | solution.py:684

commit v3 on v2

--- a/solution.py
+++ b/solution.py
@@ -437,8 +437,16 @@
             lax.fori_loop(0, ry, run(x_cell), 0)
 
 
-def slope_force(layers, cells, stride, ry, meta, spairs, cs, gd, acc_ref):
+def slope_force(
+    layers, cells, stride, ry, half, meta, spairs, cs, gd, acc_ref, slot_ref=None, values=None
+):
+    width = 2 * half
+    sub = iota((SUB, width), 0).astype(jnp.float32)
+
     def step(cell, carry):
+        if values is not None:
+            marks = slot_ref[cell // 2] - (cell % 2 * width).astype(jnp.float32)
+            found = [jnp.zeros((SUB, width), jnp.float32)] * 4
         for g in range(STATIC):
             i = cell * stride + g
             base, sp = meta[i], cs[i]
@@ -448,16 +456,26 @@
                     f = sp + spairs[slot, base + b * (ry + 1), 0]
                     for c in range(3):
                         acc[c] = acc[c] + f * gd[cell * STATIC + g, slot, b, c]
-            for c in range(3):
-                acc_ref[i, c] = acc[c]
+            if values is None:
+                for c in range(3):
+                    acc_ref[i, c] = acc[c]
+                continue
+            pick = marks == sub + float(g * SUB)
+            for c, part in enumerate(acc + [acc_ref[i, 3]]):
+                part = jnp.sum(part, axis=1, keepdims=True)
+                found[c] = found[c] + jnp.where(pick, part, 0.0)
+        if values is not None:
+            for c in range(4):
+                values[cell, c] = found[c]
         return carry
 
-    lax.fori_loop(0, cells, step, 0)
+    lax.fori_loop(0, cells, step, 0, unroll=1 if values is None else 8)
 
 
 def step_kernel(
     sizes, rx, nt, half, count_hbm, pos_hbm, slot_ref, packed, cen, pairs, vs, cs, root_ref,
-    spairs, acc_ref, count_ref, pos_ref, own, ext, raw, cent_row, meta, rho, sown, sext, gd, table, load, send, recv, send2, recv2,
+    spairs, values, count_ref, pos_ref, own, ext, raw, cent_row, meta, rho, sown, sext, gd,
+    acc_ref, table, load, send, recv, send2, recv2,
 ):
     loads = [
         pltpu.make_async_copy(count_hbm, count_ref, load.at[0]),
@@ -548,14 +566,15 @@
             arrive(e, swhere)
             build_slopes(order[e][0], rx + 2, ry, half, sext, spairs)
         layers = [order[e][0] for e in chunk]
-        slope_force(layers, cells, stride, ry, meta, spairs, cs, gd, acc_ref)
+        final = (slot_ref, values) if chunk[-1] == len(order) - 1 else ()
+        slope_force(layers, cells, stride, ry, half, meta, spairs, cs, gd, acc_ref, *final)
     wait_sends(*where)
     wait_sends(*swhere)
 
 
 def finish_kernel(
-    nz, rx, nt, half, slot_ref, packed, cen, pairs, vs, cs, root_ref, spairs, acc_ref,
-    force_ref, energy_ref, codes, values,
+    nz, rx, nt, half, slot_ref, packed, cen, pairs, vs, cs, root_ref, spairs, values,
+    force_ref, energy_ref, codes, sums,
 ):
     width, ry, tiles = 2 * half, 2 * nt, rx * nt
     stride = group_stride(half)
@@ -564,21 +583,6 @@
     for r in range(tiles):
         for k in (0, 1):
             codes[2 * r + k] = group_code(packed, r, k, half)
-
-    def gather(r, carry):
-        slot = slot_ref[r]
-        total = [jnp.zeros((SUB, width), jnp.float32) for _ in range(4)]
-        for k in (0, 1):
-            for g in range(STATIC):
-                pick = slot == sub + float(k * width + g * SUB)
-                for c in range(4):
-                    part = jnp.sum(acc_ref[(2 * r + k) * stride + g, c], axis=1, keepdims=True)
-                    total[c] = total[c] + jnp.where(pick, part, 0.0)
-        for c in range(4):
-            values[r, c] = total[c]
-        return carry
-
-    lax.fori_loop(0, tiles, gather, 0, unroll=4)
 
     def rest(cell, carry):
         r, k = cell // 2, cell % 2
@@ -597,12 +601,15 @@
                     acc[c] = acc[c] + f * dens[c] + pair[c]
                 acc[3] = acc[3] + pair[3]
             pick = slot_ref[r] == sub + (k * width + g * SUB).astype(jnp.float32)
-            for c in range(4):
-                part = jnp.sum(acc[c], axis=1, keepdims=True)
-                values[r, c] = values[r, c] + jnp.where(pick, part, 0.0)
-            return carry
-
-        lax.fori_loop(STATIC, code >> 12, group, 0)
+            parts = [jnp.sum(part, axis=1, keepdims=True) for part in acc]
+            return tuple(
+                total + jnp.where(pick, part, 0.0) for total, part in zip(carry, parts)
+            )
+
+        start = tuple(values[cell, c] for c in range(4))
+        done = lax.fori_loop(STATIC, code >> 12, group, start)
+        for c in range(4):
+            sums[cell, c] = done[c]
         return carry
 
     lax.fori_loop(0, 2 * tiles, rest, 0)
@@ -611,7 +618,7 @@
         for t in range(nt):
             r = x * nt + t
             for c in range(4):
-                value = jnp.sum(values[r, c], axis=0, keepdims=True)
+                value = jnp.sum(sums[2 * r, c] + sums[2 * r + 1, c], axis=0, keepdims=True)
                 if c < 3:
                     value = value * (4.0 / 3.0 * G2 / SCALE)
                 else:
@@ -652,7 +659,7 @@
             vmem(total, SUB, width),
             vmem(tiles, 1, width),
             vmem(layers, rows, 1, 1, width),
-            vmem(total, 4, SUB, width),
+            vmem(cells, 4, SUB, width),
     )
     held = sum(4 * math.prod(ref.shape) for ref in passed)
     shared = pl.pallas_call(
@@ -672,6 +679,7 @@
             vmem(rx, nt, 1, 1, width),
             vmem(layers, rx + 2, nt + 2, 1, 1, width),
             vmem(cells * STATIC, layers, 2, 3, SUB, width),
+            vmem(total, 4, SUB, width),
             vmem(total, 5, SUB, width),
             pltpu.SemaphoreType.DMA((2,)),
         ]
@@ -689,7 +697,7 @@
         ),
         in_specs=[VMEM] * len(passed),
         out_specs=(VMEM, VMEM),
-        scratch_shapes=[pltpu.SMEM((cells,), jnp.int32), vmem(tiles, 4, SUB, width)],
+        scratch_shapes=[pltpu.SMEM((cells,), jnp.int32), vmem(cells, 4, SUB, width)],
         compiler_params=pltpu.CompilerParams(vmem_limit_bytes=24 * 2**20),
         name="finish",
     )(*shared)

time: 24.6 us -> 24.3 us (0.988)
    pallas_call x1, Pallas kernels: 2.27 us -> 1.67 us  [body(): pl.pallas_call(functools.partial(finish_kernel, sizes[0], rx, nt, half),...]
    pallas_call x1, Pallas kernels: 21.6 us -> 21.9 us  [body(): pl.pallas_call(functools.partial(step_kernel, sizes, rx, nt, half), out_s...]
where the time goes in v3:
time: 24.3 us; the launch traced here: 24.2 us
  Pallas kernels  23.6 us (97%)
  between operations  0.64 us (3%)
    pallas_call x1, Pallas kernels, body(): pl.pallas_call(functools.partial(step_kernel, sizes, rx, nt, half), out_s...  21.9 us
    pallas_call x1, Pallas kernels, body(): pl.pallas_call(functools.partial(finish_kernel, sizes[0], rx, nt, half),...  1.67 us

profile of v3, /device:TPU:0, one launch (start us, length us, event | category | flops | bytes accessed | tf_op | source)
XLA Modules:
  0.0 24.2 jit_solution(10785930003762183235)
XLA Ops:
  0.6 21.9 %step.1 = (f32[8,1,128]{2,1,0:T(1,128)S(1)}, f32[8,1,128]{2,1,0:T(1,128)S(1)}, f32[176,3,8,128]{3,2,1,0:T(8,128)S(1)}, f32[4,36,6,1,128]{4,3,2,1,0:T(1,128)S(1)}...) custom-call(s32[1,2,8]{2,1,0:T(2,128)} %count_hbm.1, ...), custom_call_target="tpu_custom_call" | custom-call | tf_op jit(solution)/shard_map/step/pallas_call | solution.py:665
  22.6 1.7 %finish.1 = (f32[3,1,2,8,64]{4,3,2,1,0:T(8,128)}, f32[1,2,8,64]{3,2,1,0:T(8,128)}) custom-call(f32[8,1,128]{2,1,0:T(1,128)S(1)} %get-tuple-element.11.slot_ref, f32[8,1,128]{2,1,0:T(1,128)S(1)} %get-tuple-element.12.packed, f32[176,3,8,128]{3,2,1,0:T(8,128)S(1)} %get-tuple-element.13.cen, f32[4,36,6,1,128]{4,3,2,1,0:T(1,128)S(1)} %get-tuple-element.14.pairs, ...), custom_call_target="tpu_custom_call" | custom-call | tf_op jit(solution)/shard_map/finish/pallas_call | solution.py:692

commit v4 on v3

--- a/solution.py
+++ b/solution.py
@@ -326,7 +326,7 @@
             pairs[s, x * (ry + 1) + p, 0] = pair_row(rows, p, half)
         return carry
 
-    lax.fori_loop(0, cols, step, 0, unroll=2)
+    lax.fori_loop(0, cols, step, 0, unroll=4)
 
 
 def density_layer(
@@ -385,7 +385,7 @@
         sext[home, x + 1, t + 1, 0] = row
         return carry
 
-    lax.fori_loop(0, tiles, step, 0, unroll=4)
+    lax.fori_loop(0, tiles, step, 0, unroll=8)
 
 
 def pair_terms(v):
@@ -469,7 +469,7 @@
                 values[cell, c] = found[c]
         return carry
 
-    lax.fori_loop(0, cells, step, 0, unroll=1 if values is None else 8)
+    lax.fori_loop(0, cells, step, 0, unroll=2 if values is None else 8)
 
 
 def step_kernel(

time: 24.3 us -> 24.1 us (level)
  Pallas kernels: 23.6 us -> 23.2 us
where the time goes in v4:
time: 24.1 us; the launch traced here: 23.8 us
  Pallas kernels  23.2 us (96%)
  between operations  0.64 us (3%)
    pallas_call x1, Pallas kernels, body(): pl.pallas_call(functools.partial(step_kernel, sizes, rx, nt, half), out_s...  21.7 us
    pallas_call x1, Pallas kernels, body(): pl.pallas_call(functools.partial(finish_kernel, sizes[0], rx, nt, half),...  1.44 us

profile of v4, /device:TPU:0, one launch (start us, length us, event | category | flops | bytes accessed | tf_op | source)
XLA Modules:
  0.0 23.8 jit_solution(11593159088128636521)
XLA Ops:
  0.6 21.7 %step.1 = (f32[8,1,128]{2,1,0:T(1,128)S(1)}, f32[8,1,128]{2,1,0:T(1,128)S(1)}, f32[176,3,8,128]{3,2,1,0:T(8,128)S(1)}, f32[4,36,6,1,128]{4,3,2,1,0:T(1,128)S(1)}...) custom-call(s32[1,2,8]{2,1,0:T(2,128)} %count_hbm.1, ...), custom_call_target="tpu_custom_call" | custom-call | tf_op jit(solution)/shard_map/step/pallas_call | solution.py:665
  22.3 1.4 %finish.1 = (f32[3,1,2,8,64]{4,3,2,1,0:T(8,128)}, f32[1,2,8,64]{3,2,1,0:T(8,128)}) custom-call(f32[8,1,128]{2,1,0:T(1,128)S(1)} %get-tuple-element.11.slot_ref, f32[8,1,128]{2,1,0:T(1,128)S(1)} %get-tuple-element.12.packed, f32[176,3,8,128]{3,2,1,0:T(8,128)S(1)} %get-tuple-element.13.cen, f32[4,36,6,1,128]{4,3,2,1,0:T(1,128)S(1)} %get-tuple-element.14.pairs, ...), custom_call_target="tpu_custom_call" | custom-call | tf_op jit(solution)/shard_map/finish/pallas_call | solution.py:692
